TPU v7x, 256 devices: a whole 4x4x8 slice. The times are simulated.
256 devices in a mesh: fsdp: 32 (over z, y), tp: 4 (over x), job: 2 (over core).
Axes of the slice: x: 4, y: 4, z: 8, core: 2. Of those that a mesh axis runs over, the one named last changes fastest.
Arguments:
- slopes_in: float32 [1024, 128, 1024], P('job', 'fsdp', 'tp'), parts along dimension 0, may hold values from -6 to 6
- moments_in: float32 [1024, 128, 1024], P('job', 'fsdp', 'tp'), parts along dimension 0, may hold values from -6 to 6
- weights_in: float32 [1024, 128, 1024], P('job', 'fsdp', 'tp'), parts along dimension 0, may hold values from -0.1875 to 0.1875
Outputs:
- new_weights: float32 [1024, 128, 1024], P('job', 'fsdp', 'tp'), parts along dimension 0
- new_momentum: float32 [1024, 128, 1024], P('job', 'fsdp', 'tp'), parts along dimension 0
There are 2 independent parts, one for each index of `job`. A program takes and returns all parts, laid end to end along the dimension named above; each array names one. Nothing has to cross between parts.
All inputs are finite; a program needn't handle non-finite values.
Results may differ from a plain program's by a relative error of at most 0.00019.
Values sent between devices are 32-bit elements; how exact they have to be, the bound alone decides.
A program may use at most 128 MiB of HBM per device.

v0:
```python
import jax
import jax.numpy as jnp
from jax import lax
from jax.sharding import PartitionSpec as P

ITERS = 5


hold_rate = 0.9
learn_rate = 0.8


def split_up(value, dim, devices):
    lengths = value.shape
    pieces = value.reshape(*lengths[:dim], devices, lengths[dim] // devices, *lengths[dim + 1 :])
    return jnp.moveaxis(pieces, dim, 0)


def edges_of(length, count):
    unit = 8 if length >= 8 * count else 1
    return [length // unit * k // count * unit for k in range(1, count)]


def laid_out(pieces, dim):
    lengths = list(pieces.shape[1:])
    lengths[dim] *= pieces.shape[0]
    return jnp.moveaxis(pieces, 0, dim).reshape(lengths)


def cut_exchange(value, axis, pieces, split_dim, concat_dim):
    blocks = split_up(value, split_dim, lax.axis_size(axis))
    split_at = max(range(1, max(2, blocks.ndim - 1)), key=lambda d: blocks.shape[d])
    finished = []
    for share in jnp.split(blocks, edges_of(blocks.shape[split_at], pieces), axis=split_at):
        if share.size:
            finished.append(lax.all_to_all(share, axis, split_axis=0, concat_axis=0, tiled=True))
    return laid_out(jnp.concatenate(finished, axis=split_at), concat_dim)


def body(slopes_in, moments_in, weights_in):
    new_momentum = hold_rate * moments_in + slopes_in
    moved = lax.all_to_all(new_momentum, "fsdp", split_axis=0, concat_axis=1, tiled=True)
    whole = lax.all_to_all(moved, "tp", split_axis=0, concat_axis=2, tiled=True)
    iterate = whole * lax.rsqrt(jnp.sum(whole * whole, axis=(1, 2), keepdims=True) + 1e-06)
    for step in range(ITERS):
        gram = jnp.einsum("mik,mjk->mij", iterate, iterate, precision=lax.Precision.HIGHEST)
        mixed = -4.775 * gram + 2.0315 * jnp.einsum(
            "mij,mjk->mik", gram, gram, precision=lax.Precision.HIGHEST
        )
        iterate = 3.4445 * iterate + jnp.einsum(
            "mij,mjk->mik", mixed, iterate, precision=lax.Precision.HIGHEST
        )
    iterate = cut_exchange(iterate, "tp", 2, 2, 0)
    back = lax.all_to_all(iterate, "fsdp", split_axis=1, concat_axis=0, tiled=True)
    new_weights = weights_in - learn_rate * back
    return (new_weights, new_momentum)


def solution(mesh):
    placed = (P("job", "fsdp", "tp"), P("job", "fsdp", "tp"), P("job", "fsdp", "tp"))
    return jax.shard_map(
        body,
        mesh=mesh,
        in_specs=placed,
        out_specs=(P("job", "fsdp", "tp"), P("job", "fsdp", "tp")),
        check_vma=False,
    )
```

profile of v0, /device:TPU:16, one launch (start us, length us, event | category | flops | bytes accessed | tf_op | source)
XLA Modules:
  0.0 210.5 jit_solution(15059887878700993549)
XLA Ops:
  0.6 2.9 %multiply_add_fusion.5 = f32[512,4,256]{2,1,0:T(4,128)S(1)} fusion(f32[512,4,256]{2,1,0:T(4,128)} %param.3, f32[512,4,256]{2,1,0:T(4,128)} %param.4), kind=kLoop, calls=%fused_computation.9 | loop fusion | flops 1048576 | bytes 6291456 | tf_op jit(solution)/shard_map/add | solution.py:41
  3.6 0.0 copy-start
  3.6 61.9 %all_to_all.55 = f32[512,4,256]{2,1,0:T(4,128)S(1)} all-to-all(f32[512,4,256]{2,1,0:T(4,128)S(1)} %multiply_add_fusion.5), channel_id=1, replica_groups=mesh['fsdp'=32,'tp'=4,'job'=2] {'fsdp'}, dimensions={0} | all-to-all | bytes 4194304 | tf_op jit(solution)/shard_map/all_to_all | solution.py:42
  65.5 0.4 copy.20
  65.9 0.0 copy-done
  65.9 0.2 copy.21
  66.2 1.2 copy.22
  67.4 29.0 %all_to_all.56 = f32[16,128,256]{2,1,0:T(8,128)S(1)} all-to-all(f32[16,128,256]{2,1,0:T(8,128)S(1)} %copy.22), channel_id=1, replica_groups=mesh['fsdp'=32,'tp'=4,'job'=2] {'tp'}, dimensions={0} | all-to-all | bytes 4194304 | tf_op jit(solution)/shard_map/all_to_all | solution.py:43
  96.4 0.3 multiply_reduce_fusion
  96.7 0.2 copy.30
  96.9 2.3 %fusion.2 = f32[4,128,128]{2,1,0:T(8,128)S(1)} fusion(f32[4,128,1024]{2,1,0:T(8,128)S(1)} %bitcast.49, f32[4]{0:T(128)S(1)} %add_rsqrt_fusion), kind=kOutput, calls=%fused_computation.12 | convolution fusion | flops 805830656 | bytes 2359312 | tf_op jit(solution)/shard_map/mik,mjk->mij/dot_general | solution.py:46
  99.2 0.4 fusion.10
  99.6 2.1 %multiply_add_fusion.4 = f32[4,128,1024]{2,1,0:T(8,128)S(1)} fusion(f32[4,128,1024]{2,1,0:T(8,128)S(1)} %bitcast.50, f32[4,128,128]{2,1,0:T(8,128)S(1)} %fusion.10, f32[4]{0:T(128)S(1)} %add_rsqrt_fusion), kind=kOutput, calls=%fused_computation.7 | convolution fusion | flops 807403520 | bytes 4456464 | tf_op jit(solution)/shard_map/mij,mjk->mik/dot_general | solution.py:50
  101.7 2.0 fusion.14
  103.8 0.4 fusion.9
  104.1 2.1 multiply_add_fusion.3
  106.2 2.0 fusion.15
  108.3 0.4 fusion.8
  108.7 2.3 %multiply_add_fusion.2 = f32[4,128,1024]{2,1,0:T(8,128)S(1)} fusion(f32[4,128,1024]{2,1,0:T(8,128)S(1)} %multiply_add_fusion.3, f32[4,128,128]{2,1,0:T(8,128)S(1)} %fusion.8), kind=kOutput, calls=%fused_computation.5 | convolution fusion | flops 806354944 | bytes 4456448 | tf_op jit(solution)/shard_map/mij,mjk->mik/dot_general | solution.py:50
  111.0 2.0 fusion.16
  113.0 0.4 fusion.7
  113.4 2.1 multiply_add_fusion.1
  115.5 2.1 fusion.17
  117.6 0.4 fusion.6
  117.9 2.1 multiply_add_fusion
  120.0 0.2 copy.33
  120.2 0.2 fusion.13
  120.4 15.2 %all_to_all.57 = f32[4,4,64,256]{3,2,1,0:T(8,128)S(1)} all-to-all(f32[4,4,64,256]{3,2,1,0:T(8,128)S(1)} %get-tuple-element.6), channel_id=1, replica_groups=mesh['fsdp'=32,'tp'=4,'job'=2] {'tp'}, dimensions={0} | all-to-all | bytes 2097152 | tf_op jit(solution)/shard_map/all_to_all | solution.py:36
  135.6 14.3 %all_to_all.58 = f32[4,4,64,256]{3,2,1,0:T(8,128)S(1)} all-to-all(f32[4,4,64,256]{3,2,1,0:T(8,128)S(1)} %get-tuple-element.7), channel_id=1, replica_groups=mesh['fsdp'=32,'tp'=4,'job'=2] {'tp'}, dimensions={0} | all-to-all | bytes 2097152 | tf_op jit(solution)/shard_map/all_to_all | solution.py:36
  149.9 0.2 pad_maximum_fusion
  150.1 1.2 copy.25
  151.3 54.2 %all_to_all.59 = f32[16,128,256]{2,0,1:T(8,128)S(1)} all-to-all(f32[16,128,256]{2,0,1:T(8,128)S(1)} %copy.25), channel_id=1, replica_groups=mesh['fsdp'=32,'tp'=4,'job'=2] {'fsdp'}, dimensions={1} | all-to-all | bytes 4194304 | tf_op jit(solution)/shard_map/all_to_all | solution.py:54
  205.5 0.2 broadcast_multiply_fusion
  205.8 0.0 copy-start.1
  205.8 0.2 copy.26
  206.0 1.4 copy-done.1
  207.4 0.4 bitcast_subtract_fusion
  207.8 2.7 %copy.28 = f32[512,4,256]{2,1,0:T(4,128)} copy(f32[512,4,256]{2,0,1:T(8,128)S(1)} %bitcast_subtract_fusion) | data formatting | bytes 4194304
  (1 shorter events, 0.0 us)
Async XLA Ops:
  3.6 62.3 %copy-start = (f32[512,4,256]{2,1,0:T(4,128)}, f32[512,4,256]{2,1,0:T(4,128)S(1)}, u32[]{:S(2)}) copy-start(f32[512,4,256]{2,1,0:T(4,128)S(1)} %multiply_add_fusion.5) | copy-start | bytes 6291460
  205.8 1.6 copy-start.1
where the time goes:
time: 211 us; the launch traced here: 210 us
  blocking collectives  175 us (83%)
  matrix products  23 us (11%)
  local copies, waits for them, and re-layouts  7.93 us (4%)
  other arithmetic  4.11 us (2%)
    all_to_all x1, blocking collectives, body(): lax.all_to_all(new_momentum, 'fsdp', split_axis=0, concat_axis=1, tiled=T...  61.9 us
    all_to_all x1, blocking collectives, body(): lax.all_to_all(iterate, 'fsdp', split_axis=1, concat_axis=0, tiled=True)  54.2 us
    all_to_all x2, blocking collectives, cut_exchange(): lax.all_to_all(share, axis, split_axis=0, concat_axis=0, tiled=True)  29.5 us
    all_to_all x1, blocking collectives, body(): whole = lax.all_to_all(moved, 'tp', split_axis=0, concat_axis=2, tiled=True)  29 us
    dot_general x5, matrix products, body(): jnp.einsum('mij,mjk->mik', mixed, iterate, precision=lax.Precision.HIGHEST)  10.7 us
    dot_general x5, matrix products, body(): jnp.einsum('mik,mjk->mij', iterate, iterate, precision=lax.Precision.HIGH...  10.5 us

commit v1 on v0

v1 whole, which is shorter than its diff:
```python
import functools

import jax
import jax.numpy as jnp
from jax import lax
from jax.experimental import pallas as pl
from jax.experimental.pallas import tpu as pltpu
from jax.sharding import PartitionSpec as P

ITERS = 5
NZ = 8
NY = 4
NX = 4
NP = NY * NX
CHUNKS = 4

hold_rate = 0.9
learn_rate = 0.8

MESH = pl.DeviceIdType.MESH
HIGHEST = lax.Precision.HIGHEST


def dot_nn(a, b):
    return lax.dot_general(a, b, (((1,), (0,)), ((), ())), precision=HIGHEST, preferred_element_type=jnp.float32)


def dot_nt(a, b):
    return lax.dot_general(a, b, (((1,), (1,)), ((), ())), precision=HIGHEST, preferred_element_type=jnp.float32)


def kernel(
    mom, out, zin, xyin, res, xyout, xs,
    zi_send, zi_recv, pi_send, pi_recv, po_send, po_recv, zo_send, zo_recv,
):
    f, x, j = lax.axis_index("fsdp"), lax.axis_index("tp"), lax.axis_index("job")
    z, y = f // NY, lax.rem(f, NY)
    own = y * NX + x

    def along_z(d):
        return (lax.rem(z + d, NZ) * NY + y, x, j)

    def in_plane(dy, dx):
        return (z * NY + lax.rem(y + dy, NY), lax.rem(x + dx, NX), j)

    steps_z = (1, 7, 2, 6, 3, 5, 4)
    steps_p = [(dy, dx) for dx in (1, 3, 0, 2) for dy in (1, 3, 0, 2) if (dy, dx) != (0, 0)]

    barrier = pltpu.get_barrier_semaphore()
    for d in steps_z:
        pl.semaphore_signal(barrier, inc=1, device_id=along_z(d), device_id_type=MESH)
    for dy, dx in steps_p:
        pl.semaphore_signal(barrier, inc=1, device_id=in_plane(dy, dx), device_id_type=MESH)
    pl.semaphore_wait(barrier, len(steps_z) + len(steps_p))

    def send(src, dst, send_sem, recv_sem, device):
        pltpu.make_async_remote_copy(
            src_ref=src, dst_ref=dst, send_sem=send_sem, recv_sem=recv_sem, device_id=device, device_id_type=MESH
        ).start()

    def wait(ref, sem):
        pltpu.make_async_copy(ref, ref, sem).wait()

    for c in range(CHUNKS):
        for d in steps_z:
            to = lax.rem(z + d, NZ)
            send(mom.at[c, to], zin.at[c, d], zi_send.at[c], zi_recv.at[c], along_z(d))
    for c in range(CHUNKS):
        zin[c, 0] = mom[c, z]

    def plane_in(c):
        wait(zin.at[c, pl.ds(1, NZ - 1)], zi_recv.at[c])
        for dy, dx in steps_p:
            to = lax.rem(y + dy, NY) * NX + lax.rem(x + dx, NX)
            send(zin.at[c, :, to], xyin.at[c, dx * NY + dy], pi_send.at[c], pi_recv.at[c], in_plane(dy, dx))
        xyin[c, 0] = zin[c, :, own]

    def work(c):
        wait(xyin.at[c, pl.ds(1, NP - 1)], pi_recv.at[c])
        for k in range(NX):
            xs[:, k * 256 : (k + 1) * 256] = xyin[c, k * NY : (k + 1) * NY].reshape(128, 256)
        total = jnp.sum(xs[...] * xs[...])
        xs[...] = xs[...] * lax.rsqrt(jnp.full((1, 1), total, jnp.float32) + 1e-06)

        def step(_, carry):
            gram = dot_nt(xs[...], xs[...])
            mixed = -4.775 * gram + 2.0315 * dot_nn(gram, gram)
            for k in range(NX):
                part = xs[:, k * 256 : (k + 1) * 256]
                xs[:, k * 256 : (k + 1) * 256] = 3.4445 * part + dot_nn(mixed, part)
            return carry

        lax.fori_loop(0, ITERS, step, 0)
        for k in range(NX):
            res[c, k * NY : (k + 1) * NY] = xs[:, k * 256 : (k + 1) * 256].reshape(NY, NZ, 4, 256)
        xyout[c, :, own] = res[c, 0]
        for dy, dx in steps_p:
            back = in_plane(NY - dy, NX - dx)
            send(res.at[c, dx * NY + dy], xyout.at[c, :, own], po_send.at[c], po_recv.at[c], back)

    def z_out(c):
        wait(res.at[c, pl.ds(1, NP - 1)], po_recv.at[c])
        for d in steps_z:
            send(xyout.at[c, d], out.at[c, z], zo_send.at[c], zo_recv.at[c], along_z(NZ - d))
        out[c, z] = xyout[c, 0]

    def step(s, carry):
        @pl.when(s < CHUNKS)
        def _():
            plane_in(s)

        @pl.when(jnp.logical_and(s >= 1, s <= CHUNKS))
        def _():
            work(s - 1)

        @pl.when(s >= 2)
        def _():
            z_out(s - 2)

        return carry

    lax.fori_loop(0, CHUNKS + 2, step, 0)
    for c in range(CHUNKS):
        wait(zin.at[c, pl.ds(1, NZ - 1)], zo_recv.at[c])
        wait(zin.at[c, pl.ds(1, NZ - 1)], zi_send.at[c])
        wait(zin.at[c, pl.ds(1, NZ - 1)], zo_send.at[c])
        wait(xyin.at[c, pl.ds(1, NP - 1)], pi_send.at[c])
        wait(xyin.at[c, pl.ds(1, NP - 1)], po_send.at[c])


def exchange(mom):
    block = (4, 256)
    return pl.pallas_call(
        kernel,
        name="exchange",
        out_shape=jax.ShapeDtypeStruct((CHUNKS, NZ, NP, *block), jnp.float32),
        in_specs=[pl.BlockSpec(memory_space=pltpu.VMEM)],
        out_specs=pl.BlockSpec(memory_space=pltpu.VMEM),
        scratch_shapes=[
            pltpu.VMEM((CHUNKS, NZ, NP, *block), jnp.float32),
            pltpu.VMEM((CHUNKS, NP, NZ, *block), jnp.float32),
            pltpu.VMEM((CHUNKS, NP, NZ, *block), jnp.float32),
            pltpu.VMEM((CHUNKS, NZ, NP, *block), jnp.float32),
            pltpu.VMEM((128, 1024), jnp.float32),
        ]
        + [pltpu.SemaphoreType.DMA((CHUNKS,))] * 8,
        compiler_params=pltpu.CompilerParams(collective_id=0, has_side_effects=True, vmem_limit_bytes=32 * 2**20),
    )(mom)


def body(slopes_in, moments_in, weights_in):
    new_momentum = hold_rate * moments_in + slopes_in
    back = exchange(new_momentum.reshape(CHUNKS, NZ, NP, 4, 256)).reshape(slopes_in.shape)
    new_weights = weights_in - learn_rate * back
    return (new_weights, new_momentum)


def solution(mesh):
    placed = (P("job", "fsdp", "tp"), P("job", "fsdp", "tp"), P("job", "fsdp", "tp"))
    return jax.shard_map(
        body,
        mesh=mesh,
        in_specs=placed,
        out_specs=(P("job", "fsdp", "tp"), P("job", "fsdp", "tp")),
        check_vma=False,
    )
```

time: 211 us -> 111 us (0.53)
  blocking collectives: 175 us -> 0 us
  Pallas kernels: 0 us -> 104 us
  matrix products: 23 us -> 0 us
  local copies, waits for them, and re-layouts: 7.93 us -> 0.74 us
    all_to_all x5 -> x0, blocking collectives: 175 us -> none  [the longest x1 61.9 us: body(): lax.all_to_all(new_momentum, 'fsdp', split_axis=0, concat_axis=1, tiled=T...]
    pallas_call x0 -> x1, Pallas kernels: none -> 104 us  [exchange(): pl.pallas_call(kernel, name='exchange', out_shape=jax.ShapeDtypeStruct((C...]
    dot_general x15 -> x0, matrix products: 23 us -> none  [the longest x5 10.7 us: body(): jnp.einsum('mij,mjk->mik', mixed, iterate, precision=lax.Precision.HIGHEST)]
    unnamed x5 -> x4, local copies, waits for them, and re-layouts: 4.03 us -> 0.74 us
where the time goes in v1:
time: 111 us
  Pallas kernels  104 us (94%)
  other arithmetic  5.79 us (5%)
    pallas_call x1, Pallas kernels, exchange(): pl.pallas_call(kernel, name='exchange', out_shape=jax.ShapeDtypeStruct((C...  104 us
    add x1, other arithmetic, body(): new_momentum = hold_rate * moments_in + slopes_in  2.94 us

profile of v1, /device:TPU:16, one launch (start us, length us, event | category | flops | bytes accessed | tf_op | source)
XLA Modules:
  0.0 110.9 jit_solution(10804151642086716010)
XLA Ops:
  0.6 2.9 %multiply_add_fusion = f32[512,4,256]{2,1,0:T(4,128)S(1)} fusion(f32[512,4,256]{2,1,0:T(4,128)} %param.3, f32[512,4,256]{2,1,0:T(4,128)} %param.4), kind=kLoop, calls=%fused_computation.1 | loop fusion | flops 1048576 | bytes 6291456 | tf_op jit(solution)/shard_map/add | solution.py:152
  3.6 0.0 copy-start
  3.6 103.7 %exchange.1 = f32[4,8,16,4,256]{4,3,2,1,0:T(4,128)S(1)} custom-call(f32[4,8,16,4,256]{4,3,2,1,0:T(4,128)S(1)} %bitcast.3), custom_call_target="tpu_custom_call" | custom-call | tf_op jit(solution)/shard_map/exchange/pallas_call | solution.py:133
  107.3 0.0 copy-done
  107.4 0.0 copy-start.1
  107.4 0.8 broadcast_multiply_fusion
  108.2 0.7 copy-done.1
  108.9 2.0 %bitcast_subtract_fusion = f32[512,4,256]{2,1,0:T(4,128)} fusion(f32[512,4,256]{2,1,0:T(4,128)S(1)} %copy-done.1, f32[4,8,16,4,256]{4,3,2,1,0:T(4,128)S(1)} %broadcast_multiply_fusion), kind=kLoop, calls=%fused_computation | loop fusion | flops 524288 | bytes 6291456 | tf_op jit(solution)/shard_map/sub | solution.py:154
Async XLA Ops:
  3.6 103.8 %copy-start = (f32[512,4,256]{2,1,0:T(4,128)}, f32[512,4,256]{2,1,0:T(4,128)S(1)}, u32[]{:S(2)}) copy-start(f32[512,4,256]{2,1,0:T(4,128)S(1)} %multiply_add_fusion) | copy-start | bytes 6291460
  107.4 1.6 %copy-start.1 = (f32[512,4,256]{2,1,0:T(4,128)S(1)}, f32[512,4,256]{2,1,0:T(4,128)}, u32[]{:S(2)}) copy-start(f32[512,4,256]{2,1,0:T(4,128)} %param.5) | copy-start | bytes 6291460

commit v2 on v1

--- a/solution.py
+++ b/solution.py
@@ -30,8 +30,8 @@
 
 
 def kernel(
-    mom, out, zin, xyin, res, xyout, xs,
-    zi_send, zi_recv, pi_send, pi_recv, po_send, po_recv, zo_send, zo_recv,
+    slopes, moments, weights, out, mom, slopes_v, moments_v, weights_v, zin, xyin, res, xyout, xs,
+    load_s, load_m, load_w, zi_send, zi_recv, pi_send, pi_recv, po_send, po_recv, zo_send, zo_recv,
 ):
     f, x, j = lax.axis_index("fsdp"), lax.axis_index("tp"), lax.axis_index("job")
     z, y = f // NY, lax.rem(f, NY)
@@ -44,15 +44,21 @@
         return (z * NY + lax.rem(y + dy, NY), lax.rem(x + dx, NX), j)
 
     steps_z = (1, 7, 2, 6, 3, 5, 4)
+    steps_back = (4, 3, 5, 2, 6, 1, 7)
     steps_p = [(dy, dx) for dx in (1, 3, 0, 2) for dy in (1, 3, 0, 2) if (dy, dx) != (0, 0)]
 
+    loads = []
+    for c in range(CHUNKS):
+        loads.append(pltpu.make_async_copy(slopes.at[c], slopes_v.at[c], load_s.at[c]))
+        loads.append(pltpu.make_async_copy(moments.at[c], moments_v.at[c], load_m.at[c]))
+    load_weights = pltpu.make_async_copy(weights, weights_v, load_w)
+    for copy in loads:
+        copy.start()
     barrier = pltpu.get_barrier_semaphore()
     for d in steps_z:
         pl.semaphore_signal(barrier, inc=1, device_id=along_z(d), device_id_type=MESH)
     for dy, dx in steps_p:
         pl.semaphore_signal(barrier, inc=1, device_id=in_plane(dy, dx), device_id_type=MESH)
-    pl.semaphore_wait(barrier, len(steps_z) + len(steps_p))
-
     def send(src, dst, send_sem, recv_sem, device):
         pltpu.make_async_remote_copy(
             src_ref=src, dst_ref=dst, send_sem=send_sem, recv_sem=recv_sem, device_id=device, device_id_type=MESH
@@ -62,9 +68,15 @@
         pltpu.make_async_copy(ref, ref, sem).wait()
 
     for c in range(CHUNKS):
+        loads[2 * c].wait()
+        loads[2 * c + 1].wait()
+        mom[c] = hold_rate * moments_v[c] + slopes_v[c]
+        if c == 0:
+            pl.semaphore_wait(barrier, len(steps_z) + len(steps_p))
         for d in steps_z:
             to = lax.rem(z + d, NZ)
             send(mom.at[c, to], zin.at[c, d], zi_send.at[c], zi_recv.at[c], along_z(d))
+    load_weights.start()
     for c in range(CHUNKS):
         zin[c, 0] = mom[c, z]
 
@@ -92,7 +104,7 @@
 
         lax.fori_loop(0, ITERS, step, 0)
         for k in range(NX):
-            res[c, k * NY : (k + 1) * NY] = xs[:, k * 256 : (k + 1) * 256].reshape(NY, NZ, 4, 256)
+            res[c, k * NY : (k + 1) * NY] = (learn_rate * xs[:, k * 256 : (k + 1) * 256]).reshape(NY, NZ, 4, 256)
         xyout[c, :, own] = res[c, 0]
         for dy, dx in steps_p:
             back = in_plane(NY - dy, NX - dx)
@@ -100,7 +112,7 @@
 
     def z_out(c):
         wait(res.at[c, pl.ds(1, NP - 1)], po_recv.at[c])
-        for d in steps_z:
+        for d in steps_back:
             send(xyout.at[c, d], out.at[c, z], zo_send.at[c], zo_recv.at[c], along_z(NZ - d))
         out[c, z] = xyout[c, 0]
 
@@ -120,39 +132,60 @@
         return carry
 
     lax.fori_loop(0, CHUNKS + 2, step, 0)
+    load_weights.wait()
     for c in range(CHUNKS):
         wait(zin.at[c, pl.ds(1, NZ - 1)], zo_recv.at[c])
+        out[c] = weights_v[c] - out[c]
+    for c in range(CHUNKS):
         wait(zin.at[c, pl.ds(1, NZ - 1)], zi_send.at[c])
         wait(zin.at[c, pl.ds(1, NZ - 1)], zo_send.at[c])
         wait(xyin.at[c, pl.ds(1, NP - 1)], pi_send.at[c])
         wait(xyin.at[c, pl.ds(1, NP - 1)], po_send.at[c])
 
 
-def exchange(mom):
-    block = (4, 256)
-    return pl.pallas_call(
+def put_out(new_weights_v, new_momentum_v, new_weights, new_momentum, sems):
+    pairs = ((new_weights_v, new_weights), (new_momentum_v, new_momentum))
+    copies = [
+        pltpu.make_async_copy(src.at[c], dst.at[c], sems.at[i, c])
+        for c in range(CHUNKS) for i, (src, dst) in enumerate(pairs)
+    ]
+    for copy in copies:
+        copy.start()
+    for copy in copies:
+        copy.wait()
+
+
+def exchange(slopes, moments, weights):
+    shape = (CHUNKS, NZ, NP, 4, 256)
+    whole = jax.ShapeDtypeStruct(shape, jnp.float32)
+    split = pltpu.VMEM(shape, jnp.float32)
+    plane = pltpu.VMEM((CHUNKS, NP, NZ, 4, 256), jnp.float32)
+    new_weights, new_momentum = pl.pallas_call(
         kernel,
         name="exchange",
-        out_shape=jax.ShapeDtypeStruct((CHUNKS, NZ, NP, *block), jnp.float32),
-        in_specs=[pl.BlockSpec(memory_space=pltpu.VMEM)],
-        out_specs=pl.BlockSpec(memory_space=pltpu.VMEM),
-        scratch_shapes=[
-            pltpu.VMEM((CHUNKS, NZ, NP, *block), jnp.float32),
-            pltpu.VMEM((CHUNKS, NP, NZ, *block), jnp.float32),
-            pltpu.VMEM((CHUNKS, NP, NZ, *block), jnp.float32),
-            pltpu.VMEM((CHUNKS, NZ, NP, *block), jnp.float32),
-            pltpu.VMEM((128, 1024), jnp.float32),
-        ]
+        out_shape=(whole, whole),
+        in_specs=[pl.BlockSpec(memory_space=pltpu.HBM)] * 3,
+        out_specs=[pl.BlockSpec(memory_space=pltpu.VMEM)] * 2,
+        scratch_shapes=[split, split, split, split, plane, plane, split, pltpu.VMEM((128, 1024), jnp.float32)]
+        + [pltpu.SemaphoreType.DMA((CHUNKS,))] * 2
+        + [pltpu.SemaphoreType.DMA]
         + [pltpu.SemaphoreType.DMA((CHUNKS,))] * 8,
-        compiler_params=pltpu.CompilerParams(collective_id=0, has_side_effects=True, vmem_limit_bytes=32 * 2**20),
-    )(mom)
+        compiler_params=pltpu.CompilerParams(collective_id=0, has_side_effects=True, vmem_limit_bytes=40 * 2**20),
+    )(*[pltpu.with_memory_space_constraint(a.reshape(shape), pltpu.HBM) for a in (slopes, moments, weights)])
+    new_weights, new_momentum = pl.pallas_call(
+        put_out,
+        name="put_out",
+        out_shape=(whole, whole),
+        in_specs=[pl.BlockSpec(memory_space=pltpu.VMEM)] * 2,
+        out_specs=[pl.BlockSpec(memory_space=pltpu.HBM)] * 2,
+        scratch_shapes=[pltpu.SemaphoreType.DMA((2, CHUNKS))],
+        compiler_params=pltpu.CompilerParams(vmem_limit_bytes=8 * 2**20),
+    )(new_weights, new_momentum)
+    return new_weights.reshape(slopes.shape), new_momentum.reshape(slopes.shape)
 
 
 def body(slopes_in, moments_in, weights_in):
-    new_momentum = hold_rate * moments_in + slopes_in
-    back = exchange(new_momentum.reshape(CHUNKS, NZ, NP, 4, 256)).reshape(slopes_in.shape)
-    new_weights = weights_in - learn_rate * back
-    return (new_weights, new_momentum)
+    return exchange(slopes_in, moments_in, weights_in)
 
 
 def solution(mesh):

time: 111 us -> 105 us (0.946)
  other arithmetic: 5.79 us -> 0 us
    add x1 -> x0, other arithmetic: 2.94 us -> none  [body(): new_momentum = hold_rate * moments_in + slopes_in]
    sub x1 -> x0, other arithmetic: 1.99 us -> none  [body(): new_weights = weights_in - learn_rate * back]
    pallas_call x1 -> x2, Pallas kernels: 104 us -> 104 us  [the longest x1 102 us: exchange(): pl.pallas_call(kernel, name='exchange', out_shape=(whole, whole), in_spec...]
where the time goes in v2:
time: 105 us; the launch traced here: 104 us
  Pallas kernels  104 us (99%)
    pallas_call x1, Pallas kernels, exchange(): pl.pallas_call(kernel, name='exchange', out_shape=(whole, whole), in_spec...  102 us

profile of v2, /device:TPU:16, one launch (start us, length us, event | category | flops | bytes accessed | tf_op | source)
XLA Modules:
  0.0 104.3 jit_solution(209788424206043862)
XLA Ops:
  0.6 101.6 %exchange.1 = (f32[4,8,16,4,256]{4,3,2,1,0:T(4,128)S(1)}, f32[4,8,16,4,256]{4,3,2,1,0:T(4,128)S(1)}) custom-call(f32[4,8,16,4,256]{4,3,2,1,0:T(4,128)} %bitcast.5, f32[4,8,16,4,256]{4,3,2,1,0:T(4,128)} %bitcast.6, f32[4,8,16,4,256]{4,3,2,1,0:T(4,128)} %bitcast.7), custom_call_target="tpu_custom_call" | custom-call | tf_op jit(solution)/shard_map/exchange/pallas_call | solution.py:163
  102.2 2.1 %put_out.1 = (f32[4,8,16,4,256]{4,3,2,1,0:T(4,128)}, f32[4,8,16,4,256]{4,3,2,1,0:T(4,128)}) custom-call(f32[4,8,16,4,256]{4,3,2,1,0:T(4,128)S(1)} %get-tuple-element.6.new_weights_v, f32[4,8,16,4,256]{4,3,2,1,0:T(4,128)S(1)} %get-tuple-element.7.new_momentum_v), custom_call_target="tpu_custom_call" | custom-call | tf_op jit(solution)/shard_map/put_out/pallas_call | solution.py:175

commit v3 on v2

--- a/solution.py
+++ b/solution.py
@@ -18,19 +18,32 @@
 learn_rate = 0.8
 
 MESH = pl.DeviceIdType.MESH
-HIGHEST = lax.Precision.HIGHEST
 
 
 def dot_nn(a, b):
-    return lax.dot_general(a, b, (((1,), (0,)), ((), ())), precision=HIGHEST, preferred_element_type=jnp.float32)
+    return lax.dot_general(a, b, (((1,), (0,)), ((), ())), preferred_element_type=jnp.float32)
 
 
 def dot_nt(a, b):
-    return lax.dot_general(a, b, (((1,), (1,)), ((), ())), precision=HIGHEST, preferred_element_type=jnp.float32)
+    return lax.dot_general(a, b, (((1,), (1,)), ((), ())), preferred_element_type=jnp.float32)
+
+
+def thirds(v):
+    high = v.astype(jnp.bfloat16)
+    rest = v - high.astype(jnp.float32)
+    mid = rest.astype(jnp.bfloat16)
+    return high, mid, (rest - mid.astype(jnp.float32)).astype(jnp.bfloat16)
+
+
+def product(a, b):
+    left = jnp.concatenate([a[0], a[1]], axis=1)
+    ends = jnp.concatenate([a[0], a[2]], axis=1)
+    small = dot_nn(ends, jnp.concatenate([b[2], b[0]], axis=0)) + dot_nn(left, jnp.concatenate([b[1], b[1]], axis=0))
+    return small + dot_nn(left, jnp.concatenate([b[0], b[0]], axis=0))
 
 
 def kernel(
-    slopes, moments, weights, out, mom, slopes_v, moments_v, weights_v, zin, xyin, res, xyout, xs,
+    slopes, moments, weights, out, mom, slopes_v, moments_v, weights_v, zin, xyin, res, xyout, xs, top, low,
     load_s, load_m, load_w, zi_send, zi_recv, pi_send, pi_recv, po_send, po_recv, zo_send, zo_recv,
 ):
     f, x, j = lax.axis_index("fsdp"), lax.axis_index("tp"), lax.axis_index("job")
@@ -95,11 +108,17 @@
         xs[...] = xs[...] * lax.rsqrt(jnp.full((1, 1), total, jnp.float32) + 1e-06)
 
         def step(_, carry):
-            gram = dot_nt(xs[...], xs[...])
-            mixed = -4.775 * gram + 2.0315 * dot_nn(gram, gram)
             for k in range(NX):
-                part = xs[:, k * 256 : (k + 1) * 256]
-                xs[:, k * 256 : (k + 1) * 256] = 3.4445 * part + dot_nn(mixed, part)
+                at = slice(k * 256, (k + 1) * 256)
+                top[0:128, at], top[128:256, at], low[:, at] = thirds(xs[:, at])
+            upper = dot_nt(top[0:128], top[...])
+            mixed_terms = upper[:, 128:] + dot_nt(top[0:128], low[...])
+            gram = upper[:, :128] + (dot_nt(top[128:256], top[128:256]) + mixed_terms + mixed_terms.T)
+            parts = thirds(gram)
+            mixed = thirds(-4.775 * gram + 2.0315 * product(parts, parts))
+            for k in range(NX):
+                at = slice(k * 256, (k + 1) * 256)
+                xs[:, at] = 3.4445 * xs[:, at] + product(mixed, (top[0:128, at], top[128:256, at], low[:, at]))
             return carry
 
         lax.fori_loop(0, ITERS, step, 0)
@@ -167,6 +186,7 @@
         in_specs=[pl.BlockSpec(memory_space=pltpu.HBM)] * 3,
         out_specs=[pl.BlockSpec(memory_space=pltpu.VMEM)] * 2,
         scratch_shapes=[split, split, split, split, plane, plane, split, pltpu.VMEM((128, 1024), jnp.float32)]
+        + [pltpu.VMEM((256, 1024), jnp.bfloat16), pltpu.VMEM((128, 1024), jnp.bfloat16)]
         + [pltpu.SemaphoreType.DMA((CHUNKS,))] * 2
         + [pltpu.SemaphoreType.DMA]
         + [pltpu.SemaphoreType.DMA((CHUNKS,))] * 8,

time: 105 us -> 105 us (level)
  no operation moved by 1% of the time
where the time goes in v3:
time: 105 us; the launch traced here: 103 us
  Pallas kernels  103 us (98%)
    pallas_call x1, Pallas kernels, exchange(): pl.pallas_call(kernel, name='exchange', out_shape=(whole, whole), in_spec...  101 us

profile of v3, /device:TPU:16, one launch (start us, length us, event | category | flops | bytes accessed | tf_op | source)
XLA Modules:
  0.0 103.2 jit_solution(15971745251158962290)
XLA Ops:
  0.6 100.5 %exchange.1 = (f32[4,8,16,4,256]{4,3,2,1,0:T(4,128)S(1)}, f32[4,8,16,4,256]{4,3,2,1,0:T(4,128)S(1)}) custom-call(f32[4,8,16,4,256]{4,3,2,1,0:T(4,128)} %bitcast.5, f32[4,8,16,4,256]{4,3,2,1,0:T(4,128)} %bitcast.6, f32[4,8,16,4,256]{4,3,2,1,0:T(4,128)} %bitcast.7), custom_call_target="tpu_custom_call" | custom-call | tf_op jit(solution)/shard_map/exchange/pallas_call | solution.py:182
  101.1 2.1 %put_out.1 = (f32[4,8,16,4,256]{4,3,2,1,0:T(4,128)}, f32[4,8,16,4,256]{4,3,2,1,0:T(4,128)}) custom-call(f32[4,8,16,4,256]{4,3,2,1,0:T(4,128)S(1)} %get-tuple-element.6.new_weights_v, f32[4,8,16,4,256]{4,3,2,1,0:T(4,128)S(1)} %get-tuple-element.7.new_momentum_v), custom_call_target="tpu_custom_call" | custom-call | tf_op jit(solution)/shard_map/put_out/pallas_call | solution.py:195

commit v4 on v3

--- a/solution.py
+++ b/solution.py
@@ -44,7 +44,7 @@
 
 def kernel(
     slopes, moments, weights, out, mom, slopes_v, moments_v, weights_v, zin, xyin, res, xyout, xs, top, low,
-    load_s, load_m, load_w, zi_send, zi_recv, pi_send, pi_recv, po_send, po_recv, zo_send, zo_recv,
+    round_sem, load_s, load_m, load_w, zi_send, zi_recv, pi_send, pi_recv, po_send, po_recv, zo_send, zo_recv,
 ):
     f, x, j = lax.axis_index("fsdp"), lax.axis_index("tp"), lax.axis_index("job")
     z, y = f // NY, lax.rem(f, NY)
@@ -65,13 +65,20 @@
         loads.append(pltpu.make_async_copy(slopes.at[c], slopes_v.at[c], load_s.at[c]))
         loads.append(pltpu.make_async_copy(moments.at[c], moments_v.at[c], load_m.at[c]))
     load_weights = pltpu.make_async_copy(weights, weights_v, load_w)
-    for copy in loads:
+    for copy in loads[:2]:
         copy.start()
     barrier = pltpu.get_barrier_semaphore()
-    for d in steps_z:
-        pl.semaphore_signal(barrier, inc=1, device_id=along_z(d), device_id_type=MESH)
-    for dy, dx in steps_p:
-        pl.semaphore_signal(barrier, inc=1, device_id=in_plane(dy, dx), device_id_type=MESH)
+    near = [along_z(1), along_z(NZ - 1), in_plane(1, 0), in_plane(NY - 1, 0), in_plane(0, 1), in_plane(0, NX - 1)]
+    for device in near:
+        pl.semaphore_signal(barrier, inc=1, device_id=device, device_id_type=MESH)
+
+    def tell(k):
+        for device in near:
+            pl.semaphore_signal(round_sem.at[k], inc=1, device_id=device, device_id_type=MESH)
+
+    def hear(k):
+        pl.semaphore_wait(round_sem.at[k], len(near))
+
     def send(src, dst, send_sem, recv_sem, device):
         pltpu.make_async_remote_copy(
             src_ref=src, dst_ref=dst, send_sem=send_sem, recv_sem=recv_sem, device_id=device, device_id_type=MESH
@@ -80,15 +87,36 @@
     def wait(ref, sem):
         pltpu.make_async_copy(ref, ref, sem).wait()
 
-    for c in range(CHUNKS):
+    def send_in(c, d):
+        send(mom.at[c, lax.rem(z + d, NZ)], zin.at[c, d], zi_send.at[c], zi_recv.at[c], along_z(d))
+
+    def momentum(c):
         loads[2 * c].wait()
         loads[2 * c + 1].wait()
         mom[c] = hold_rate * moments_v[c] + slopes_v[c]
-        if c == 0:
-            pl.semaphore_wait(barrier, len(steps_z) + len(steps_p))
+
+    pl.semaphore_wait(barrier, len(near))
+    tell(0)
+    momentum(0)
+    for copy in loads[2:]:
+        copy.start()
+    send_in(0, 1)
+    send_in(0, NZ - 1)
+    hear(0)
+    tell(1)
+    send_in(0, 2)
+    send_in(0, NZ - 2)
+    hear(1)
+    tell(2)
+    send_in(0, 3)
+    send_in(0, NZ - 3)
+    for c in range(1, CHUNKS):
+        momentum(c)
+    hear(2)
+    send_in(0, 4)
+    for c in range(1, CHUNKS):
         for d in steps_z:
-            to = lax.rem(z + d, NZ)
-            send(mom.at[c, to], zin.at[c, d], zi_send.at[c], zi_recv.at[c], along_z(d))
+            send_in(c, d)
     load_weights.start()
     for c in range(CHUNKS):
         zin[c, 0] = mom[c, z]
@@ -187,6 +215,7 @@
         out_specs=[pl.BlockSpec(memory_space=pltpu.VMEM)] * 2,
         scratch_shapes=[split, split, split, split, plane, plane, split, pltpu.VMEM((128, 1024), jnp.float32)]
         + [pltpu.VMEM((256, 1024), jnp.bfloat16), pltpu.VMEM((128, 1024), jnp.bfloat16)]
+        + [pltpu.SemaphoreType.REGULAR((3,))]
         + [pltpu.SemaphoreType.DMA((CHUNKS,))] * 2
         + [pltpu.SemaphoreType.DMA]
         + [pltpu.SemaphoreType.DMA((CHUNKS,))] * 8,

time: 105 us -> 104 us (level)
  no operation moved by 1% of the time
where the time goes in v4:
time: 104 us; the launch traced here: 102 us
  Pallas kernels  102 us (98%)
    pallas_call x1, Pallas kernels, exchange(): pl.pallas_call(kernel, name='exchange', out_shape=(whole, whole), in_spec...  99.7 us

profile of v4, /device:TPU:16, one launch (start us, length us, event | category | flops | bytes accessed | tf_op | source)
XLA Modules:
  0.0 102.4 jit_solution(13646453176886831864)
XLA Ops:
  0.6 99.7 %exchange.1 = (f32[4,8,16,4,256]{4,3,2,1,0:T(4,128)S(1)}, f32[4,8,16,4,256]{4,3,2,1,0:T(4,128)S(1)}) custom-call(f32[4,8,16,4,256]{4,3,2,1,0:T(4,128)} %bitcast.5, f32[4,8,16,4,256]{4,3,2,1,0:T(4,128)} %bitcast.6, f32[4,8,16,4,256]{4,3,2,1,0:T(4,128)} %bitcast.7), custom_call_target="tpu_custom_call" | custom-call | tf_op jit(solution)/shard_map/exchange/pallas_call | solution.py:210
  100.4 2.1 %put_out.1 = (f32[4,8,16,4,256]{4,3,2,1,0:T(4,128)}, f32[4,8,16,4,256]{4,3,2,1,0:T(4,128)}) custom-call(f32[4,8,16,4,256]{4,3,2,1,0:T(4,128)S(1)} %get-tuple-element.6.new_weights_v, f32[4,8,16,4,256]{4,3,2,1,0:T(4,128)S(1)} %get-tuple-element.7.new_momentum_v), custom_call_target="tpu_custom_call" | custom-call | tf_op jit(solution)/shard_map/put_out/pallas_call | solution.py:224

commit v5 on v4

--- a/solution.py
+++ b/solution.py
@@ -43,7 +43,7 @@
 
 
 def kernel(
-    slopes, moments, weights, out, mom, slopes_v, moments_v, weights_v, zin, xyin, res, xyout, xs, top, low,
+    slopes, moments, weights, out, mom, last_w, slopes_v, moments_v, weights_v, zin, xyin, res, xyout, xs, top, low,
     round_sem, load_s, load_m, load_w, zi_send, zi_recv, pi_send, pi_recv, po_send, po_recv, zo_send, zo_recv,
 ):
     f, x, j = lax.axis_index("fsdp"), lax.axis_index("tp"), lax.axis_index("job")
@@ -64,7 +64,8 @@
     for c in range(CHUNKS):
         loads.append(pltpu.make_async_copy(slopes.at[c], slopes_v.at[c], load_s.at[c]))
         loads.append(pltpu.make_async_copy(moments.at[c], moments_v.at[c], load_m.at[c]))
-    load_weights = pltpu.make_async_copy(weights, weights_v, load_w)
+    load_weights = pltpu.make_async_copy(weights.at[pl.ds(0, CHUNKS - 1)], weights_v, load_w.at[0])
+    load_last = pltpu.make_async_copy(weights.at[CHUNKS - 1], last_w, load_w.at[1])
     for copy in loads[:2]:
         copy.start()
     barrier = pltpu.get_barrier_semaphore()
@@ -110,14 +111,14 @@
     tell(2)
     send_in(0, 3)
     send_in(0, NZ - 3)
-    for c in range(1, CHUNKS):
-        momentum(c)
     hear(2)
     send_in(0, 4)
     for c in range(1, CHUNKS):
+        momentum(c)
         for d in steps_z:
             send_in(c, d)
     load_weights.start()
+    load_last.start()
     for c in range(CHUNKS):
         zin[c, 0] = mom[c, z]
 
@@ -180,9 +181,11 @@
 
     lax.fori_loop(0, CHUNKS + 2, step, 0)
     load_weights.wait()
+    load_last.wait()
     for c in range(CHUNKS):
         wait(zin.at[c, pl.ds(1, NZ - 1)], zo_recv.at[c])
-        out[c] = weights_v[c] - out[c]
+        if c < CHUNKS - 1:
+            out[c] = weights_v[c] - out[c]
     for c in range(CHUNKS):
         wait(zin.at[c, pl.ds(1, NZ - 1)], zi_send.at[c])
         wait(zin.at[c, pl.ds(1, NZ - 1)], zo_send.at[c])
@@ -190,16 +193,18 @@
         wait(xyin.at[c, pl.ds(1, NP - 1)], po_send.at[c])
 
 
-def put_out(new_weights_v, new_momentum_v, new_weights, new_momentum, sems):
-    pairs = ((new_weights_v, new_weights), (new_momentum_v, new_momentum))
-    copies = [
-        pltpu.make_async_copy(src.at[c], dst.at[c], sems.at[i, c])
-        for c in range(CHUNKS) for i, (src, dst) in enumerate(pairs)
-    ]
+def put_out(new_weights_v, new_momentum_v, last_w, new_weights, new_momentum, last_v, sems):
+    final = CHUNKS - 1
+    copies = [pltpu.make_async_copy(new_weights_v.at[c], new_weights.at[c], sems.at[0, c]) for c in range(final)]
+    copies += [pltpu.make_async_copy(new_momentum_v.at[c], new_momentum.at[c], sems.at[1, c]) for c in range(CHUNKS)]
     for copy in copies:
         copy.start()
+    last_v[...] = last_w[...] - new_weights_v[final]
+    last_copy = pltpu.make_async_copy(last_v, new_weights.at[final], sems.at[0, final])
+    last_copy.start()
     for copy in copies:
         copy.wait()
+    last_copy.wait()
 
 
 def exchange(slopes, moments, weights):
@@ -207,17 +212,18 @@
     whole = jax.ShapeDtypeStruct(shape, jnp.float32)
     split = pltpu.VMEM(shape, jnp.float32)
     plane = pltpu.VMEM((CHUNKS, NP, NZ, 4, 256), jnp.float32)
-    new_weights, new_momentum = pl.pallas_call(
+    chunk = jax.ShapeDtypeStruct(shape[1:], jnp.float32)
+    new_weights, new_momentum, last = pl.pallas_call(
         kernel,
         name="exchange",
-        out_shape=(whole, whole),
+        out_shape=(whole, whole, chunk),
         in_specs=[pl.BlockSpec(memory_space=pltpu.HBM)] * 3,
-        out_specs=[pl.BlockSpec(memory_space=pltpu.VMEM)] * 2,
-        scratch_shapes=[split, split, split, split, plane, plane, split, pltpu.VMEM((128, 1024), jnp.float32)]
+        out_specs=[pl.BlockSpec(memory_space=pltpu.VMEM)] * 3,
+        scratch_shapes=[split, split, pltpu.VMEM((CHUNKS - 1, *shape[1:]), jnp.float32), split, plane, plane, split, pltpu.VMEM((128, 1024), jnp.float32)]
         + [pltpu.VMEM((256, 1024), jnp.bfloat16), pltpu.VMEM((128, 1024), jnp.bfloat16)]
         + [pltpu.SemaphoreType.REGULAR((3,))]
         + [pltpu.SemaphoreType.DMA((CHUNKS,))] * 2
-        + [pltpu.SemaphoreType.DMA]
+        + [pltpu.SemaphoreType.DMA((2,))]
         + [pltpu.SemaphoreType.DMA((CHUNKS,))] * 8,
         compiler_params=pltpu.CompilerParams(collective_id=0, has_side_effects=True, vmem_limit_bytes=40 * 2**20),
     )(*[pltpu.with_memory_space_constraint(a.reshape(shape), pltpu.HBM) for a in (slopes, moments, weights)])
@@ -225,11 +231,11 @@
         put_out,
         name="put_out",
         out_shape=(whole, whole),
-        in_specs=[pl.BlockSpec(memory_space=pltpu.VMEM)] * 2,
+        in_specs=[pl.BlockSpec(memory_space=pltpu.VMEM)] * 3,
         out_specs=[pl.BlockSpec(memory_space=pltpu.HBM)] * 2,
-        scratch_shapes=[pltpu.SemaphoreType.DMA((2, CHUNKS))],
+        scratch_shapes=[pltpu.VMEM(shape[1:], jnp.float32), pltpu.SemaphoreType.DMA((2, CHUNKS))],
         compiler_params=pltpu.CompilerParams(vmem_limit_bytes=8 * 2**20),
-    )(new_weights, new_momentum)
+    )(new_weights, new_momentum, last)
     return new_weights.reshape(slopes.shape), new_momentum.reshape(slopes.shape)
 
 

time: 104 us -> 104 us (level)
  no operation moved by 1% of the time
where the time goes in v5:
time: 104 us; the launch traced here: 102 us
  Pallas kernels  102 us (98%)
    pallas_call x1, Pallas kernels, exchange(): pl.pallas_call(kernel, name='exchange', out_shape=(whole, whole, chunk),...  99.7 us

profile of v5, /device:TPU:16, one launch (start us, length us, event | category | flops | bytes accessed | tf_op | source)
XLA Modules:
  0.0 102.4 jit_solution(15153073593683887231)
XLA Ops:
  0.6 99.7 %exchange.1 = (f32[4,8,16,4,256]{4,3,2,1,0:T(4,128)S(1)}, f32[4,8,16,4,256]{4,3,2,1,0:T(4,128)S(1)}, f32[8,16,4,256]{3,2,1,0:T(4,128)S(1)}) custom-call(f32[4,8,16,4,256]{4,3,2,1,0:T(4,128)} %bitcast.5, f32[4,8,16,4,256]{4,3,2,1,0:T(4,128)} %bitcast.6, f32[4,8,16,4,256]{4,3,2,1,0:T(4,128)} %bitcast.7), custom_call_target="tpu_custom_call" | custom-call | tf_op jit(solution)/shard_map/exchange/pallas_call | solution.py:216
  100.3 2.1 %put_out.1 = (f32[4,8,16,4,256]{4,3,2,1,0:T(4,128)}, f32[4,8,16,4,256]{4,3,2,1,0:T(4,128)}) custom-call(f32[4,8,16,4,256]{4,3,2,1,0:T(4,128)S(1)} %get-tuple-element.7.new_weights_v, f32[4,8,16,4,256]{4,3,2,1,0:T(4,128)S(1)} %get-tuple-element.8.new_momentum_v, f32[8,16,4,256]{3,2,1,0:T(4,128)S(1)} %get-tuple-element.9.last_w), custom_call_target="tpu_custom_call" | custom-call | tf_op jit(solution)/shard_map/put_out/pallas_call | solution.py:230
